TPU v7x, 32 devices: a whole 2x2x4 slice. The times are simulated.
32 devices in a mesh: grp: 4 (over z), seq: 4 (over y, x), mp: 2 (over core).
Axes of the slice: x: 2, y: 2, z: 4, core: 2. Of those that a mesh axis runs over, the one named last changes fastest.
Arguments:
- queries: bfloat16 [4, 1024, 2048], P('grp', 'seq', 'mp'), may hold values from -400 to 400
- neighbours: bfloat16 [4, 16, 256, 1024], P('grp', 'seq'), may hold values from -6 to 6
- w_key: bfloat16 [1024, 2048], P(('grp', 'seq'), 'mp'), may hold values from -0.1875 to 0.1875
- w_value: bfloat16 [1024, 2048], P(('grp', 'seq'), 'mp'), may hold values from -0.1875 to 0.1875
- lambdas: float32 [16], P('mp'), may hold values from 0.2 to 0.9
- gain: float32 [2048], P('mp'), may hold values from 0.5 to 1.5
- counts: int32 [4], P('grp'), may hold values from 2 to 16, as said below
- d_out: bfloat16 [4, 1024, 2048], P('grp', 'seq', 'mp'), may hold values from -6 to 6
Outputs:
- attended: bfloat16 [4, 1024, 2048], P('grp', 'seq', 'mp')
- d_neigh: float32 [4, 16, 256, 1024], P('grp', 'seq', None, 'mp')
Inputs may be any that keep to these rules, and one draw needn't show every extreme that they name: `counts`: at least one sequence has all 16 groups valid.
All inputs are finite; a program needn't handle non-finite values.
Results may differ from a plain program's by a relative error of at most 0.017.
Values may be sent and summed in bfloat16 or wider, within the bound.
A program may use at most 128 MiB of HBM per device.

v0:
```python
import functools

import jax
import jax.numpy as jnp
from jax import lax
from jax.experimental import pallas as pl
from jax.experimental.pallas import tpu as pltpu
from jax.sharding import PartitionSpec as P

EPSILON = 1e-06
MESH = pl.DeviceIdType.MESH
NT = (((1,), (1,)), ((), ()))
TN = (((0,), (0,)), ((), ()))


def dot(left, right, dims=(((1,), (0,)), ((), ()))):
    return lax.dot_general(left, right, dims, preferred_element_type=jnp.float32)


def kernel(
    sizes,
    lambdas,
    counts,
    q_hbm,
    n_hbm,
    wk_hbm,
    wv_hbm,
    gain,
    do_hbm,
    att,
    d_out,
    x,
    q,
    do,
    wk,
    wv,
    acc,
    send,
    got,
    edge,
    local_sem,
    own_sem,
    x_send,
    x_recv,
    p1_send,
    p1_recv,
    p2_send,
    p2_recv,
    g_send,
    g_recv,
    e_send,
    e_recv,
):
    n_grp, n_seq, n_mp, w_seq, chunks, pairs = sizes
    groups, rows, enc = x.shape
    group_len = q.shape[0] // groups
    cols = wk.shape[-1]
    pair_cols = cols // pairs
    head_dim = pair_cols // 2
    half = enc // n_mp
    grp, seq, mp = lax.axis_index("grp"), lax.axis_index("seq"), lax.axis_index("mp")
    w_pos = seq if w_seq > 1 else 0
    following = lax.rem(seq + 1, n_seq)
    preceding = lax.rem(seq + n_seq - 1, n_seq)

    own = []
    for c in range(chunks):
        for kind, (src, dst) in enumerate(((wk_hbm, wk), (wv_hbm, wv))):
            own.append(
                pltpu.make_async_copy(
                    src.at[:, pl.ds(c * cols, cols)], dst.at[c, grp, w_pos], own_sem.at[c, kind]
                )
            )
    for copy in own:
        copy.start()
    local = [
        pltpu.make_async_copy(n_hbm.at[pl.ds(0, groups - 1)], x.at[pl.ds(1, groups - 1)], local_sem.at[0]),
        pltpu.make_async_copy(q_hbm, q, local_sem.at[1]),
        pltpu.make_async_copy(do_hbm, do, local_sem.at[2]),
    ]
    for copy in local:
        copy.start()

    others = [{"grp": lax.rem(grp + o, n_grp)} for o in range(1, n_grp)]
    others += [{"seq": lax.rem(seq + o, n_seq)} for o in (range(1, n_seq) if w_seq > 1 else (1, n_seq - 1))]
    for o in range(1, n_mp):
        partner = lax.rem(mp + o, n_mp)
        others += [{"mp": partner}, {"seq": following, "mp": partner}, {"seq": preceding, "mp": partner}]
    barrier = pltpu.get_barrier_semaphore()
    for device in others:
        pl.semaphore_signal(barrier, inc=1, device_id=device, device_id_type=MESH)
    pl.semaphore_wait(barrier, len(others))

    def remote(src, dst, send_sem, recv_sem, device):
        return pltpu.make_async_remote_copy(
            src_ref=src, dst_ref=dst, send_sem=send_sem, recv_sem=recv_sem, device_id=device, device_id_type=MESH
        )

    def over_grp(sems, c, kind, block):
        return [
            remote(block, block, sems[0].at[c, kind, o], sems[1].at[c, kind, o], {"grp": lax.rem(grp + o, n_grp)})
            for o in range(1, n_grp)
        ]

    def over_seq(sems, c, kind, block):
        return [
            remote(block, block, sems[0].at[c, kind, o], sems[1].at[c, kind, o], {"seq": lax.rem(seq + o, n_seq)})
            for o in range(1, w_seq)
        ]

    first, second, onward = [], [], []
    for c in range(chunks):
        early, late, relay = [], [], []
        for kind, ref in enumerate((wk, wv)):
            early += over_grp((p1_send, p1_recv), c, kind, ref.at[c, grp, w_pos])
            block = ref.at[c, :, w_pos]
            if w_seq == 4:
                right = lax.rem(seq, 2) * 2 + 1 - seq // 2
                left = (1 - lax.rem(seq, 2)) * 2 + seq // 2
                for o, device in ((1, right), (2, left)):
                    late.append(
                        remote(block, block, p2_send.at[c, kind, o], p2_recv.at[c, kind, o], {"seq": device})
                    )
                source, target = (left, right) if kind == 0 else (right, left)
                passed = ref.at[c, :, source]
                relay.append(
                    (
                        late[2 * kind + kind],
                        remote(passed, passed, p2_send.at[c, kind, 3], p2_recv.at[c, kind, 3], {"seq": target}),
                    )
                )
            else:
                late += over_seq((p2_send, p2_recv), c, kind, block)
        first.append(early)
        second.append(late)
        onward.append(relay)
    part = pl.ds(pl.multiple_of(mp * (rows // n_mp), rows // n_mp), rows // n_mp)
    edge_in = remote(n_hbm.at[groups - 1, part], x.at[0, part], x_send.at[0], x_recv.at[0], {"seq": following})
    edge_on = [
        remote(x.at[0, part], x.at[0, part], x_send.at[o], x_recv.at[o], {"mp": lax.rem(mp + o, n_mp)})
        for o in range(1, n_mp)
    ]

    def start_first(c):
        if c < chunks:
            own[2 * c].wait()
            own[2 * c + 1].wait()
            for copy in first[c]:
                copy.start()

    def start_second(c):
        if c < chunks:
            for copy in first[c]:
                copy.wait_recv()
            for copy in second[c]:
                copy.start()
            start_first(c + 2)

    def start_onward(c):
        if c < chunks:
            for arrival, copy in onward[c]:
                arrival.wait_recv()
                copy.start()

    def arrived(c):
        passed_on = [arrival for arrival, _ in onward[c]]
        for copy in second[c] + [copy for _, copy in onward[c]]:
            if not any(copy is other for other in passed_on):
                copy.wait_recv()
        start_second(c + 2)
        start_onward(c + 1)

    start_first(0)
    edge_in.start()
    start_first(1)
    start_second(0)
    edge_in.wait_recv()
    for copy in edge_on:
        copy.start()
    start_second(1)
    start_onward(0)
    for copy in local:
        copy.wait()
    for copy in edge_on:
        copy.wait_recv()

    scale = head_dim ** (-0.5)
    lane = lax.broadcasted_iota(jnp.int32, (group_len, pair_cols), 1)
    on_first = lane < head_dim

    def slot_step(c, u):
        w_k = wk[c].reshape(enc, cols)
        w_v = wv[c].reshape(enc, cols)
        enc_rows = x[u]
        keys = dot(enc_rows, w_k)
        vals = dot(enc_rows, w_v).astype(jnp.bfloat16)
        position = seq * groups + u
        active = (jnp.clip(position, 0, 1) * jnp.clip(counts[0] - position, 0, 1)).astype(jnp.float32)
        tokens = pl.ds(pl.multiple_of(u * group_len, group_len), group_len)
        d_keys, d_vals = [], []
        for p in range(pairs):
            at = pl.ds((c * pairs + p) * pair_cols, pair_cols)
            here = slice(p * pair_cols, (p + 1) * pair_cols)
            lam = lambdas[c * pairs + p]
            query = q[tokens, at]
            zero = jnp.zeros_like(query)
            q2 = jnp.concatenate([jnp.where(on_first, query, zero), jnp.where(on_first, zero, query)], axis=0)
            key = keys[:, here]
            value = vals[:, here]
            key_hi = key.astype(jnp.bfloat16)
            key_lo = (key - key_hi.astype(jnp.float32)).astype(jnp.bfloat16)
            scores = (
                dot(jnp.concatenate([q2, q2], axis=1), jnp.concatenate([key_hi, key_lo], axis=1), NT) * scale
            )
            top = jnp.max(scores, axis=-1, keepdims=True)
            e = jnp.exp(scores - top)
            probs = e * (1.0 / jnp.sum(e, axis=-1, keepdims=True))
            mix = (probs[:group_len] - lam * probs[group_len:]).astype(jnp.bfloat16)
            heads = dot(mix, value)
            inverse = lax.rsqrt(jnp.mean(heads * heads, axis=-1, keepdims=True) + EPSILON)
            normed = heads * inverse
            g = gain[:, at]
            att[tokens, at] = (normed * g * active).astype(jnp.bfloat16)
            dn = do[tokens, at].astype(jnp.float32) * active * g
            d_heads = (inverse * (dn - normed * jnp.mean(dn * normed, axis=-1, keepdims=True))).astype(jnp.bfloat16)
            d_mix = dot(d_heads, value, NT)
            d_vals.append(dot(mix, d_heads, TN).astype(jnp.bfloat16))
            d_probs = jnp.concatenate([d_mix, -lam * d_mix], axis=0)
            total = jnp.sum(d_probs * probs, axis=-1, keepdims=True)
            d_scores = (scale * probs * (d_probs - total)).astype(jnp.bfloat16)
            d_keys.append(dot(d_scores, q2, TN).astype(jnp.bfloat16))
        grad = dot(jnp.concatenate(d_keys, axis=1), w_k, NT) + dot(jnp.concatenate(d_vals, axis=1), w_v, NT)
        if c == 0:
            acc[u] = grad
        else:
            acc[u] += grad

    for c in range(chunks - 1):
        arrived(c)

        def step(u, carry, c=c):
            slot_step(c, u)
            return carry

        lax.fori_loop(0, groups, step, 0)

    last = chunks - 1
    arrived(last)
    mine = pl.ds(pl.multiple_of(mp * half, half), half)

    slot_step(last, 0)
    edge_out = []
    for o in range(n_mp):
        core = lax.rem(mp + o, n_mp)
        send[0, o] = acc[0, :, pl.ds(pl.multiple_of(core * half, half), half)].astype(jnp.bfloat16)
        edge_out.append(
            remote(send.at[0, o], edge.at[o], e_send.at[o], e_recv.at[o], {"seq": preceding, "mp": core})
        )
    for copy in edge_out:
        copy.start()

    def exchange(u, o):
        return remote(
            send.at[u, o], got.at[u, o], g_send.at[u, o], g_recv.at[u, o], {"mp": lax.rem(mp + o, n_mp)}
        )

    def last_step(u, carry):
        slot_step(last, u)
        for o in range(1, n_mp):
            core = lax.rem(mp + o, n_mp)
            send[u, o] = acc[u, :, pl.ds(pl.multiple_of(core * half, half), half)].astype(jnp.bfloat16)
            exchange(u, o).start()
        return carry

    lax.fori_loop(1, groups, last_step, 0)

    for copy in edge_out:
        copy.wait()
    total = edge[0].astype(jnp.float32)
    for o in range(1, n_mp):
        total += edge[o].astype(jnp.float32)
    d_out[groups - 1] = total

    def finish(u, carry):
        total = acc[u, :, mine]
        for o in range(1, n_mp):
            exchange(u, o).wait()
            total += got[u, o].astype(jnp.float32)
        d_out[u - 1] = total
        return carry

    lax.fori_loop(1, groups, finish, 0)
    for c in range(chunks):
        for copy in first[c] + second[c] + [copy for _, copy in onward[c]]:
            copy.wait_send()
    edge_in.wait_send()
    for copy in edge_on:
        copy.wait_send()


def on_device(mesh_shape, queries, neighbours, w_key, w_value, lambdas, gain, counts, d_out):
    n_grp, n_seq, n_mp = (mesh_shape[name] for name in ("grp", "seq", "mp"))
    groups, rows, enc = neighbours.shape[1:]
    tokens, width = queries.shape[1:]
    w_seq = n_seq
    if w_key.shape[0] % 16:
        w_key = lax.all_gather(w_key, "seq", axis=0, tiled=True)
        w_value = lax.all_gather(w_value, "seq", axis=0, tiled=True)
        w_seq = 1
    w_rows = w_key.shape[0]
    pair_count = lambdas.shape[0]
    pairs = 2 if pair_count % 2 == 0 else 1
    chunks = pair_count // pairs
    cols = w_key.shape[1] // chunks
    half = enc // n_mp
    bf16, f32 = jnp.bfloat16, jnp.float32
    vmem = pl.BlockSpec(memory_space=pltpu.VMEM)
    smem = pl.BlockSpec(memory_space=pltpu.SMEM)
    hbm = pl.BlockSpec(memory_space=pl.ANY)
    dma = pltpu.SemaphoreType.DMA
    att, d_neigh = pl.pallas_call(
        functools.partial(kernel, (n_grp, n_seq, n_mp, w_seq, chunks, pairs)),
        out_shape=(
            jax.ShapeDtypeStruct((tokens, width), bf16),
            jax.ShapeDtypeStruct((groups, rows, half), f32),
        ),
        in_specs=[smem, smem, hbm, hbm, hbm, hbm, vmem, hbm],
        out_specs=(vmem, vmem),
        scratch_shapes=[
            pltpu.VMEM((groups, rows, enc), bf16),
            pltpu.VMEM((tokens, width), bf16),
            pltpu.VMEM((tokens, width), bf16),
            pltpu.VMEM((chunks, n_grp, w_seq, w_rows, cols), bf16),
            pltpu.VMEM((chunks, n_grp, w_seq, w_rows, cols), bf16),
            pltpu.VMEM((groups, rows, enc), f32),
            pltpu.VMEM((groups, n_mp, rows, half), bf16),
            pltpu.VMEM((groups, n_mp, rows, half), bf16),
            pltpu.VMEM((n_mp, rows, half), bf16),
            dma((3,)),
            dma((chunks, 2)),
            dma((n_mp,)),
            dma((n_mp,)),
            dma((chunks, 2, max(n_grp, w_seq))),
            dma((chunks, 2, max(n_grp, w_seq))),
            dma((chunks, 2, max(n_grp, w_seq))),
            dma((chunks, 2, max(n_grp, w_seq))),
            dma((groups, n_mp)),
            dma((groups, n_mp)),
            dma((n_mp,)),
            dma((n_mp,)),
        ],
        compiler_params=pltpu.CompilerParams(
            collective_id=0, has_side_effects=True, vmem_limit_bytes=60 * 1024 * 1024
        ),
    )(lambdas, counts, queries[0], neighbours[0], w_key, w_value, gain.reshape(1, -1), d_out[0])
    return att[None], d_neigh[None]


def solution(mesh):
    in_specs = (
        P("grp", "seq", "mp"),
        P("grp", "seq", None, None),
        P(("grp", "seq"), "mp"),
        P(("grp", "seq"), "mp"),
        P("mp"),
        P("mp"),
        P("grp"),
        P("grp", "seq", "mp"),
    )
    out_specs = (P("grp", "seq", "mp"), P("grp", "seq", None, "mp"))
    return jax.shard_map(
        functools.partial(on_device, dict(mesh.shape)),
        mesh=mesh,
        in_specs=in_specs,
        out_specs=out_specs,
        check_vma=False,
    )
```

profile of v0, /device:TPU:27, one launch (start us, length us, event | category | flops | bytes accessed | tf_op | source)
XLA Modules:
  0.0 84.2 jit_solution(2422407525021547754)
XLA Ops:
  1.3 78.0 %shard_map.95 = (bf16[256,1024]{1,0:T(8,128)(2,1)}, f32[4,256,512]{2,1,0:T(8,128)}) custom-call(f32[8]{0:T(128)} %lambdas.1, s32[1]{0:T(128)S(6)} %copy.12.counts, bf16[256,1024]{1,0:T(8,128)(2,1)} %bitcast.8, bf16[4,256,1024]{2,1,0:T(8,128)(2,1)} %bitcast.6, bf16[64,1024]{1,0:T(8,128)(2,1)} %wk_hbm.1, bf16[64,1024]{1,0:T(8,128)(2,1)} %wv_hbm.1, ...), custom_call_target="tpu_custom_call" | custom-call | tf_op jit(solution)/shard_map/pallas_call | solution.py:321
  79.3 1.9 %copy.13 = bf16[1,256,1024]{2,1,0:T(8,128)(2,1)} copy(bf16[1,256,1024]{2,1,0:T(8,128)(2,1)} %bitcast.10) | data formatting | bytes 1048576
  81.2 3.1 %copy.14 = f32[1,4,256,512]{3,2,1,0:T(8,128)} copy(f32[1,4,256,512]{3,2,1,0:T(8,128)} %bitcast.7) | data formatting | bytes 4194304
where the time goes:
time: 84.5 us; the launch traced here: 84.2 us
  Pallas kernels  78 us (92%)
  local copies, waits for them, and re-layouts  4.95 us (6%)
  between operations  1.29 us (2%)
    pallas_call x1, Pallas kernels, on_device(): pl.pallas_call(functools.partial(kernel, (n_grp, n_seq, n_mp, w_seq, chun...  78 us
    unnamed x2, local copies, waits for them, and re-layouts  4.95 us

commit v1 on v0

v1 whole, which is shorter than its diff:
```python
import functools

import jax
import jax.numpy as jnp
from jax import lax
from jax.experimental import pallas as pl
from jax.experimental.pallas import tpu as pltpu
from jax.sharding import PartitionSpec as P

EPSILON = 1e-06
MESH = pl.DeviceIdType.MESH
NT = (((1,), (1,)), ((), ()))
TN = (((0,), (0,)), ((), ()))


def dot(left, right, dims=(((1,), (0,)), ((), ()))):
    return lax.dot_general(left, right, dims, preferred_element_type=jnp.float32)


def kernel(
    sizes,
    lambdas,
    counts,
    q_hbm,
    n_hbm,
    wk_hbm,
    wv_hbm,
    gain,
    do_hbm,
    att,
    d_out,
    x,
    qd,
    edge,
    w,
    acc,
    key,
    value,
    d_kv,
    att_out,
    att_in,
    send,
    got,
    local_sem,
    own_sem,
    z_send,
    z_recv,
    s_send,
    s_recv,
    r_send,
    r_recv,
    e_send,
    e_recv,
    a_send,
    a_recv,
    g_send,
    g_recv,
):
    n_grp, n_seq, n_mp, w_seq, chunks = sizes
    groups, rows, enc = x.shape
    group_len = qd.shape[1] // groups
    cols = w.shape[-1] // 2
    head_dim = cols // 2
    half = enc // n_mp
    grp_half = n_grp // n_mp
    grp, seq, mp = lax.axis_index("grp"), lax.axis_index("seq"), lax.axis_index("mp")
    w_pos = seq if w_seq > 1 else 0
    following = lax.rem(seq + 1, n_seq)
    preceding = lax.rem(seq + n_seq - 1, n_seq)
    ring = w_seq == 4
    if ring:
        right = lax.rem(seq, 2) * 2 + 1 - seq // 2
        left = (1 - lax.rem(seq, 2)) * 2 + seq // 2

    def at(c):
        return pl.ds(pl.multiple_of(c * cols, cols), cols)

    def own(c):
        return [
            pltpu.make_async_copy(
                src.at[:, at(c)], w.at[c, grp, w_pos, :, pl.ds(kind * cols, cols)], own_sem.at[c, kind]
            )
            for kind, src in enumerate((wk_hbm, wv_hbm))
        ]

    for c in range(chunks):
        for copy in own(c):
            copy.start()
    local = [
        pltpu.make_async_copy(q_hbm, qd.at[0], local_sem.at[0]),
        pltpu.make_async_copy(do_hbm, qd.at[1], local_sem.at[1]),
        pltpu.make_async_copy(n_hbm, x, local_sem.at[2]),
    ]
    for copy in local:
        copy.start()

    others = [{"grp": lax.rem(grp + o, n_grp)} for o in range(1, n_grp)]
    others += [{"seq": lax.rem(seq + o, n_seq)} for o in (range(1, n_seq) if w_seq > 1 else (1, n_seq - 1))]
    others += [{"mp": lax.rem(mp + o, n_mp)} for o in range(1, n_mp)]
    barrier = pltpu.get_barrier_semaphore()
    for device in others:
        pl.semaphore_signal(barrier, inc=1, device_id=device, device_id_type=MESH)
    pl.semaphore_wait(barrier, len(others))

    def remote(src, dst, send_sem, recv_sem, device):
        return pltpu.make_async_remote_copy(
            src_ref=src, dst_ref=dst, send_sem=send_sem, recv_sem=recv_sem, device_id=device, device_id_type=MESH
        )

    def over_grp(c):
        block = w.at[c, grp, w_pos]
        return [
            remote(block, block, z_send.at[c, o], z_recv.at[c, o], {"grp": lax.rem(grp + o, n_grp)})
            for o in range(1, n_grp)
        ]

    def over_seq(c):
        block = w.at[c, :, w_pos]
        if ring:
            targets = (right, left)
        else:
            targets = [lax.rem(seq + o, n_seq) for o in range(1, w_seq)]
        return [
            remote(block, block, s_send.at[c, i], s_recv.at[c, i], {"seq": target})
            for i, target in enumerate(targets)
        ]

    def relay(c):
        if not ring:
            return []
        copies = []
        for i, (source, target) in enumerate(((left, right), (right, left))):
            passed = w.at[c, :, source, :, pl.ds(i * cols, cols)]
            copies.append(remote(passed, passed, r_send.at[c, i], r_recv.at[c, i], {"seq": target}))
        return copies

    def edge_in(c):
        return remote(
            qd.at[:, pl.ds(0, group_len), at(c)],
            edge.at[:, :, at(c)],
            e_send.at[c],
            e_recv.at[c],
            {"seq": preceding},
        )

    def edge_out(c):
        return remote(
            att_out.at[:, at(c)], att_in.at[:, at(c)], a_send.at[c], a_recv.at[c], {"seq": following}
        )

    def start_grp(c):
        for copy in own(c):
            copy.wait()
        for copy in over_grp(c):
            copy.start()

    def start_seq(c):
        for copy in over_grp(c):
            copy.wait_recv()
        for copy in over_seq(c):
            copy.start()

    def start_relay(c):
        for arrival in over_seq(c):
            arrival.wait_recv()
        for copy in relay(c):
            copy.start()

    def start_edge(c):
        @pl.when(seq > 0)
        def _():
            edge_in(c).start()

    def arrived(c):
        for copy in relay(c):
            copy.wait_recv()

        @pl.when(seq < n_seq - 1)
        def _():
            edge_in(c).wait_recv()

    start_grp(0)
    start_grp(1)
    for copy in local[:2]:
        copy.wait()
    start_edge(0)
    start_edge(1)
    start_grp(2)

    @pl.when(seq == n_seq - 1)
    def _():
        edge[...] = jnp.zeros_like(edge)

    @pl.when(seq == 0)
    def _():
        att_in[...] = jnp.zeros_like(att_in)

    start_seq(0)
    acc[...] = jnp.zeros_like(acc)
    start_seq(1)
    start_relay(0)
    local[2].wait()

    scale = head_dim ** (-0.5)
    lane = lax.broadcasted_iota(jnp.int32, (group_len, cols), 1)
    on_first = lane < head_dim
    lane_row = lax.broadcasted_iota(jnp.int32, (1, 2 * group_len), 1)

    def project(c):
        weights = w[c].reshape(enc, 2 * cols)
        kv = dot(x[...].reshape(groups * rows, enc), weights)
        k = kv[:, :cols]
        hi = k.astype(jnp.bfloat16)
        key[:, :cols] = hi
        key[:, cols:] = (k - hi.astype(jnp.float32)).astype(jnp.bfloat16)
        value[...] = kv[:, cols:].astype(jnp.bfloat16)

    def attend(c, u):
        here = slice(u * rows, (u + 1) * rows)
        position = seq * groups + u + 1
        active = jnp.clip(counts[0] - position, 0, 1).astype(jnp.float32)
        lam = lambdas[c]
        if u < groups - 1:
            tokens = slice((u + 1) * group_len, (u + 2) * group_len)
            query = qd[0, tokens, at(c)]
            upstream = qd[1, tokens, at(c)]
        else:
            query = edge[0, :, at(c)]
            upstream = edge[1, :, at(c)]
        zero = jnp.zeros_like(query)
        q2 = jnp.concatenate([jnp.where(on_first, query, zero), jnp.where(on_first, zero, query)], axis=0)
        v = value[here, :]
        scores = dot(key[here, :], jnp.concatenate([q2, q2], axis=1), NT) * scale
        e = jnp.exp(scores - jnp.max(scores, axis=0, keepdims=True))
        weight = jnp.where(lane_row < group_len, jnp.float32(1.0), -lam)
        probs = e * (weight / jnp.sum(e, axis=0, keepdims=True))
        mix = (probs + pltpu.roll(probs, group_len, 1)).astype(jnp.bfloat16)
        heads = dot(mix, v, TN)[:group_len]
        inverse = lax.rsqrt(jnp.mean(heads * heads, axis=-1, keepdims=True) + EPSILON)
        normed = heads * inverse
        g = gain[:, at(c)]
        result = (normed * g * active).astype(jnp.bfloat16)
        if u < groups - 1:
            att[tokens, at(c)] = result
        else:
            att_out[:, at(c)] = result
        dn = upstream.astype(jnp.float32) * active * g
        d_heads = (inverse * (dn - normed * jnp.mean(dn * normed, axis=-1, keepdims=True))).astype(jnp.bfloat16)
        d_mix = dot(v, jnp.concatenate([d_heads, d_heads], axis=0), NT)
        total = jnp.sum(d_mix * probs, axis=0, keepdims=True) * (1.0 / weight)
        d_scores = (scale * probs * (d_mix - total)).astype(jnp.bfloat16)
        blank = jnp.zeros_like(q2)
        other = jnp.concatenate([d_heads, jnp.zeros_like(d_heads)], axis=0)
        right_side = jnp.concatenate(
            [jnp.concatenate([q2, blank], axis=1), jnp.concatenate([blank, other], axis=1)], axis=0
        )
        d_kv[here, :] = dot(jnp.concatenate([d_scores, mix], axis=1), right_side).astype(jnp.bfloat16)

    def weight_part(c, core):
        part = w[c, pl.ds(core * grp_half, grp_half)]
        return part.reshape(half, 2 * cols)

    def gradients(c):
        for core in range(n_mp):
            acc[core] += dot(d_kv[...], weight_part(c, core), NT)

    def step(c, first=False, final=False):
        if not final:

            @pl.when(c + 2 < chunks)
            def _():
                start_seq(c + 2)
                start_edge(c + 2)

            @pl.when(c + 3 < chunks)
            def _():
                start_grp(c + 3)

        arrived(c)
        project(c)
        if not final:
            start_relay(c + 1)
        if not first:
            gradients(c - 1)

            @pl.when(seq < n_seq - 1)
            def _():
                edge_out(c - 1).start()

        for u in range(groups):
            attend(c, u)

    step(0, first=True)

    def loop(c, carry):
        step(c)
        return carry

    lax.fori_loop(1, chunks - 1, loop, 0)
    last = chunks - 1
    step(last, final=True)

    pieces = send.shape[1]
    piece = send.shape[2]

    def exchange(o, i):
        return remote(
            send.at[o - 1, i], got.at[o - 1, i], g_send.at[o, i], g_recv.at[o, i], {"mp": lax.rem(mp + o, n_mp)}
        )

    for o in range(1, n_mp):
        core = lax.rem(mp + o, n_mp)
        for i in range(pieces):
            span = slice(i * piece, (i + 1) * piece)
            part = acc[core, span, :] + dot(d_kv[span, :], weight_part(last, core), NT)
            send[o - 1, i] = part.astype(jnp.bfloat16)
            exchange(o, i).start()

    @pl.when(seq < n_seq - 1)
    def _():
        edge_out(last).start()

    d_out[...] = acc[mp] + dot(d_kv[...], weight_part(last, mp), NT)

    @pl.when(seq > 0)
    def _():
        for c in range(chunks):
            edge_out(c).wait_recv()

    att[:group_len, :] = att_in[...]
    for i in range(pieces):
        span = slice(i * piece, (i + 1) * piece)
        total = d_out[span, :]
        for o in range(1, n_mp):
            exchange(o, i).wait()
            total += got[o - 1, i].astype(jnp.float32)
        d_out[span, :] = total

    def drain(c, carry):
        for copy in over_grp(c) + over_seq(c) + relay(c):
            copy.wait_send()

        @pl.when(seq > 0)
        def _():
            edge_in(c).wait_send()

        @pl.when(seq < n_seq - 1)
        def _():
            edge_out(c).wait_send()

        return carry

    lax.fori_loop(0, chunks, drain, 0)


def put_out(att, d_neigh, att_hbm, d_hbm, sem):
    copies = [
        pltpu.make_async_copy(d_neigh, d_hbm, sem.at[0]),
        pltpu.make_async_copy(att, att_hbm, sem.at[1]),
    ]
    for copy in copies:
        copy.start()
    for copy in copies:
        copy.wait()


def on_device(mesh_shape, queries, neighbours, w_key, w_value, lambdas, gain, counts, d_out):
    n_grp, n_seq, n_mp = (mesh_shape[name] for name in ("grp", "seq", "mp"))
    groups, rows, enc = neighbours.shape[1:]
    tokens, width = queries.shape[1:]
    w_seq = n_seq
    if w_key.shape[0] % 16:
        w_key = lax.all_gather(w_key, "seq", axis=0, tiled=True)
        w_value = lax.all_gather(w_value, "seq", axis=0, tiled=True)
        w_seq = 1
    w_rows = w_key.shape[0]
    chunks = lambdas.shape[0]
    cols = w_key.shape[1] // chunks
    half = enc // n_mp
    group_len = tokens // groups
    pieces = 2
    bf16, f32 = jnp.bfloat16, jnp.float32
    vmem = pl.BlockSpec(memory_space=pltpu.VMEM)
    smem = pl.BlockSpec(memory_space=pltpu.SMEM)
    hbm = pl.BlockSpec(memory_space=pl.ANY)
    dma = pltpu.SemaphoreType.DMA
    hops = max(2, w_seq)
    att, d_neigh = pl.pallas_call(
        functools.partial(kernel, (n_grp, n_seq, n_mp, w_seq, chunks)),
        out_shape=(
            pltpu.VMEM((tokens, width), bf16),
            pltpu.VMEM((groups * rows, half), f32),
        ),
        in_specs=[smem, smem, hbm, hbm, hbm, hbm, vmem, hbm],
        out_specs=(vmem, vmem),
        scratch_shapes=[
            pltpu.VMEM((groups, rows, enc), bf16),
            pltpu.VMEM((2, tokens, width), bf16),
            pltpu.VMEM((2, group_len, width), bf16),
            pltpu.VMEM((chunks, n_grp, w_seq, w_rows, 2 * cols), bf16),
            pltpu.VMEM((n_mp, groups * rows, half), f32),
            pltpu.VMEM((groups * rows, 2 * cols), bf16),
            pltpu.VMEM((groups * rows, cols), bf16),
            pltpu.VMEM((groups * rows, 2 * cols), bf16),
            pltpu.VMEM((group_len, width), bf16),
            pltpu.VMEM((group_len, width), bf16),
            pltpu.VMEM((n_mp - 1, pieces, groups * rows // pieces, half), bf16),
            pltpu.VMEM((n_mp - 1, pieces, groups * rows // pieces, half), bf16),
            dma((3,)),
            dma((chunks, 2)),
            dma((chunks, n_grp)),
            dma((chunks, n_grp)),
            dma((chunks, hops)),
            dma((chunks, hops)),
            dma((chunks, 2)),
            dma((chunks, 2)),
            dma((chunks,)),
            dma((chunks,)),
            dma((chunks,)),
            dma((chunks,)),
            dma((n_mp, pieces)),
            dma((n_mp, pieces)),
        ],
        compiler_params=pltpu.CompilerParams(
            collective_id=0, has_side_effects=True, vmem_limit_bytes=48 * 1024 * 1024
        ),
    )(lambdas, counts, queries[0], neighbours[0], w_key, w_value, gain.reshape(1, -1), d_out[0])
    att, d_neigh = pl.pallas_call(
        put_out,
        out_shape=(
            jax.ShapeDtypeStruct((tokens, width), bf16),
            jax.ShapeDtypeStruct((groups * rows, half), f32),
        ),
        in_specs=[vmem, vmem],
        out_specs=(hbm, hbm),
        scratch_shapes=[dma((2,))],
        compiler_params=pltpu.CompilerParams(vmem_limit_bytes=1024 * 1024),
    )(att, d_neigh)
    return att[None], d_neigh.reshape(1, groups, rows, half)


def solution(mesh):
    in_specs = (
        P("grp", "seq", "mp"),
        P("grp", "seq", None, None),
        P(("grp", "seq"), "mp"),
        P(("grp", "seq"), "mp"),
        P("mp"),
        P("mp"),
        P("grp"),
        P("grp", "seq", "mp"),
    )
    out_specs = (P("grp", "seq", "mp"), P("grp", "seq", None, "mp"))
    return jax.shard_map(
        functools.partial(on_device, dict(mesh.shape)),
        mesh=mesh,
        in_specs=in_specs,
        out_specs=out_specs,
        check_vma=False,
    )
```

time: 84.5 us -> 83.7 us (level)
  the two profiles are of different devices: /device:TPU:27 before, /device:TPU:0 now
where the time goes in v1:
time: 83.7 us; the launch traced here: 83.3 us
  Pallas kernels  75.2 us (90%)
  local copies, waits for them, and re-layouts  6.81 us (8%)
  between operations  1.3 us (2%)
    pallas_call x1, Pallas kernels, on_device(): pl.pallas_call(functools.partial(kernel, (n_grp, n_seq, n_mp, w_seq, chun...  73.7 us
    unnamed x14, local copies, waits for them, and re-layouts  6.81 us

profile of v1, /device:TPU:0, one launch (start us, length us, event | category | flops | bytes accessed | tf_op | source)
XLA Modules:
  0.0 83.3 jit_solution(5632755340200035188)
XLA Ops:
  1.3 0.0 copy-start
  1.3 1.6 %copy-done = bf16[1,4,256,1024]{3,2,1,0:T(8,128)(2,1)S(1)} copy-done((bf16[1,4,256,1024]{3,2,1,0:T(8,128)(2,1)S(1)}, bf16[1,4,256,1024]{3,2,1,0:T(8,128)(2,1)}, u32[]{:S(2)}) %copy-start) | copy-done | bytes 2097176
  2.9 0.0 copy-start.1
  2.9 1.0 %copy-done.1 = bf16[1,256,1024]{2,1,0:T(8,128)(2,1)S(1)} copy-done((bf16[1,256,1024]{2,1,0:T(8,128)(2,1)S(1)}, bf16[1,256,1024]{2,1,0:T(8,128)(2,1)}, u32[]{:S(2)}) %copy-start.1) | copy-done | bytes 524312
  3.9 0.0 copy-start.2
  3.9 1.0 %copy-done.2 = bf16[1,256,1024]{2,1,0:T(8,128)(2,1)S(1)} copy-done((bf16[1,256,1024]{2,1,0:T(8,128)(2,1)S(1)}, bf16[1,256,1024]{2,1,0:T(8,128)(2,1)}, u32[]{:S(2)}) %copy-start.2) | copy-done | bytes 524312
  5.0 0.0 copy-start.3
  5.0 0.9 %copy-done.3 = bf16[64,1024]{1,0:T(8,128)(2,1)S(1)} copy-done((bf16[64,1024]{1,0:T(8,128)(2,1)S(1)}, bf16[64,1024]{1,0:T(8,128)(2,1)}, u32[]{:S(2)}) %copy-start.3) | copy-done | bytes 131096
  5.9 0.0 copy-start.4
  5.9 0.9 %copy-done.4 = bf16[64,1024]{1,0:T(8,128)(2,1)S(1)} copy-done((bf16[64,1024]{1,0:T(8,128)(2,1)S(1)}, bf16[64,1024]{1,0:T(8,128)(2,1)}, u32[]{:S(2)}) %copy-start.4) | copy-done | bytes 131096
  6.8 0.0 copy-start.5
  6.8 0.7 copy-done.5
  7.5 0.0 copy-start.6
  7.5 0.7 copy-done.6
  8.1 73.7 %shard_map.95 = (bf16[256,1024]{1,0:T(8,128)(2,1)S(1)}, f32[1024,512]{1,0:T(8,128)S(1)}) custom-call(f32[8]{0:T(128)S(1)} %copy-done.6, s32[1]{0:T(128)S(6)} %copy.10.counts, bf16[256,1024]{1,0:T(8,128)(2,1)S(1)} %bitcast.7, bf16[4,256,1024]{2,1,0:T(8,128)(2,1)S(1)} %bitcast.6, bf16[64,1024]{1,0:T(8,128)(2,1)S(1)} %copy-done.3, ...), custom_call_target="tpu_custom_call" | custom-call | tf_op jit(solution)/shard_map/pallas_call | solution.py:388
  81.8 1.5 %shard_map.96 = (bf16[256,1024]{1,0:T(8,128)(2,1)}, f32[1024,512]{1,0:T(8,128)}) custom-call(bf16[256,1024]{1,0:T(8,128)(2,1)S(1)} %get-tuple-element.6.att, f32[1024,512]{1,0:T(8,128)S(1)} %get-tuple-element.7.d_neigh), custom_call_target="tpu_custom_call" | custom-call | tf_op jit(solution)/shard_map/pallas_call | solution.py:428
Async XLA Ops:
  1.3 1.6 %copy-start = (bf16[1,4,256,1024]{3,2,1,0:T(8,128)(2,1)S(1)}, bf16[1,4,256,1024]{3,2,1,0:T(8,128)(2,1)}, u32[]{:S(2)}) copy-start(bf16[1,4,256,1024]{3,2,1,0:T(8,128)(2,1)} %param.9) | copy-start | bytes 6291460
  2.9 1.0 %copy-start.1 = (bf16[1,256,1024]{2,1,0:T(8,128)(2,1)S(1)}, bf16[1,256,1024]{2,1,0:T(8,128)(2,1)}, u32[]{:S(2)}) copy-start(bf16[1,256,1024]{2,1,0:T(8,128)(2,1)} %param.8) | copy-start | bytes 1572868
  3.9 1.0 %copy-start.2 = (bf16[1,256,1024]{2,1,0:T(8,128)(2,1)S(1)}, bf16[1,256,1024]{2,1,0:T(8,128)(2,1)}, u32[]{:S(2)}) copy-start(bf16[1,256,1024]{2,1,0:T(8,128)(2,1)} %param.15) | copy-start | bytes 1572868
  5.0 0.9 %copy-start.3 = (bf16[64,1024]{1,0:T(8,128)(2,1)S(1)}, bf16[64,1024]{1,0:T(8,128)(2,1)}, u32[]{:S(2)}) copy-start(bf16[64,1024]{1,0:T(8,128)(2,1)} %wk_hbm.1) | copy-start | bytes 393220
  5.9 0.9 %copy-start.4 = (bf16[64,1024]{1,0:T(8,128)(2,1)S(1)}, bf16[64,1024]{1,0:T(8,128)(2,1)}, u32[]{:S(2)}) copy-start(bf16[64,1024]{1,0:T(8,128)(2,1)} %wv_hbm.1) | copy-start | bytes 393220
  6.8 0.7 copy-start.5
  7.5 0.7 copy-start.6

commit v2 on v1

--- a/solution.py
+++ b/solution.py
@@ -8,6 +8,7 @@
 from jax.sharding import PartitionSpec as P
 
 EPSILON = 1e-06
+TOGETHER = 4
 MESH = pl.DeviceIdType.MESH
 NT = (((1,), (1,)), ((), ()))
 TN = (((0,), (0,)), ((), ()))
@@ -107,30 +108,32 @@
             src_ref=src, dst_ref=dst, send_sem=send_sem, recv_sem=recv_sem, device_id=device, device_id_type=MESH
         )
 
-    def over_grp(c):
-        block = w.at[c, grp, w_pos]
+    if ring:
+        targets = (right, left)
+    else:
+        targets = [lax.rem(seq + o, n_seq) for o in range(1, w_seq)]
+    hops = range(1, n_grp)
+    by_grp = chunks - 1 if ring and chunks > 4 else chunks
+
+    def over_grp(c, whole=False):
+        block = w.at[c, grp] if whole else w.at[c, grp, w_pos]
         return [
-            remote(block, block, z_send.at[c, o], z_recv.at[c, o], {"grp": lax.rem(grp + o, n_grp)})
-            for o in range(1, n_grp)
+            remote(block, block, z_send.at[c, o], z_recv.at[c, o], {"grp": lax.rem(grp + o, n_grp)}) for o in hops
         ]
 
-    def over_seq(c):
-        block = w.at[c, :, w_pos]
-        if ring:
-            targets = (right, left)
-        else:
-            targets = [lax.rem(seq + o, n_seq) for o in range(1, w_seq)]
+    def over_seq(c, o):
+        block = w.at[c, lax.rem(grp + n_grp - o, n_grp), w_pos]
         return [
-            remote(block, block, s_send.at[c, i], s_recv.at[c, i], {"seq": target})
+            remote(block, block, s_send.at[c, i, o], s_recv.at[c, i, o], {"seq": target})
             for i, target in enumerate(targets)
         ]
 
-    def relay(c):
+    def relay(c, grps=slice(None)):
         if not ring:
             return []
         copies = []
         for i, (source, target) in enumerate(((left, right), (right, left))):
-            passed = w.at[c, :, source, :, pl.ds(i * cols, cols)]
+            passed = w.at[c, grps, source, :, pl.ds(i * cols, cols)]
             copies.append(remote(passed, passed, r_send.at[c, i], r_recv.at[c, i], {"seq": target}))
         return copies
 
@@ -148,44 +151,49 @@
             att_out.at[:, at(c)], att_in.at[:, at(c)], a_send.at[c], a_recv.at[c], {"seq": following}
         )
 
-    def start_grp(c):
-        for copy in own(c):
-            copy.wait()
-        for copy in over_grp(c):
+    def start(copies):
+        for copy in copies:
             copy.start()
 
+    def received(copies):
+        for copy in copies:
+            copy.wait_recv()
+
     def start_seq(c):
-        for copy in over_grp(c):
-            copy.wait_recv()
-        for copy in over_seq(c):
-            copy.start()
+        for o, arrival in zip(hops, over_grp(c)):
+            arrival.wait_recv()
+            start(over_seq(c, o))
 
     def start_relay(c):
-        for arrival in over_seq(c):
-            arrival.wait_recv()
-        for copy in relay(c):
-            copy.start()
+        for o in range(n_grp):
+            received(over_seq(c, o))
+        start(relay(c))
 
     def start_edge(c):
         @pl.when(seq > 0)
         def _():
             edge_in(c).start()
 
-    def arrived(c):
-        for copy in relay(c):
-            copy.wait_recv()
+    def arrived(c, whole=False):
+        if whole:
+            received(over_grp(c, True))
+        else:
+            received(relay(c))
 
         @pl.when(seq < n_seq - 1)
         def _():
             edge_in(c).wait_recv()
 
-    start_grp(0)
-    start_grp(1)
+    for c in [*range(by_grp, chunks), *range(by_grp)]:
+        for copy in own(c):
+            copy.wait()
+        if c < by_grp:
+            start(over_grp(c))
+        start(over_seq(c, 0))
     for copy in local[:2]:
         copy.wait()
-    start_edge(0)
-    start_edge(1)
-    start_grp(2)
+    for c in range(min(3, chunks)):
+        start_edge(c)
 
     @pl.when(seq == n_seq - 1)
     def _():
@@ -195,10 +203,19 @@
     def _():
         att_in[...] = jnp.zeros_like(att_in)
 
+    acc[...] = jnp.zeros_like(acc)
+    for c in range(by_grp, chunks):
+        received(over_seq(c, 0))
+        start(relay(c, grp))
     start_seq(0)
-    acc[...] = jnp.zeros_like(acc)
-    start_seq(1)
+    for c in range(by_grp, chunks):
+        received(relay(c, grp))
+        start(over_grp(c, True))
+    if by_grp > 1:
+        start_seq(1)
     start_relay(0)
+    if by_grp > 2:
+        start_seq(2)
     local[2].wait()
 
     scale = head_dim ** (-0.5)
@@ -208,53 +225,66 @@
 
     def project(c):
         weights = w[c].reshape(enc, 2 * cols)
-        kv = dot(x[...].reshape(groups * rows, enc), weights)
+        states = x[...].reshape(groups * rows, enc)
+        kv = dot(states[:, : enc // 2], weights[: enc // 2]) + dot(states[:, enc // 2 :], weights[enc // 2 :])
         k = kv[:, :cols]
         hi = k.astype(jnp.bfloat16)
         key[:, :cols] = hi
         key[:, cols:] = (k - hi.astype(jnp.float32)).astype(jnp.bfloat16)
         value[...] = kv[:, cols:].astype(jnp.bfloat16)
 
-    def attend(c, u):
-        here = slice(u * rows, (u + 1) * rows)
-        position = seq * groups + u + 1
-        active = jnp.clip(counts[0] - position, 0, 1).astype(jnp.float32)
+    def attend(c, slots):
         lam = lambdas[c]
-        if u < groups - 1:
-            tokens = slice((u + 1) * group_len, (u + 2) * group_len)
-            query = qd[0, tokens, at(c)]
-            upstream = qd[1, tokens, at(c)]
-        else:
-            query = edge[0, :, at(c)]
-            upstream = edge[1, :, at(c)]
-        zero = jnp.zeros_like(query)
-        q2 = jnp.concatenate([jnp.where(on_first, query, zero), jnp.where(on_first, zero, query)], axis=0)
-        v = value[here, :]
-        scores = dot(key[here, :], jnp.concatenate([q2, q2], axis=1), NT) * scale
-        e = jnp.exp(scores - jnp.max(scores, axis=0, keepdims=True))
         weight = jnp.where(lane_row < group_len, jnp.float32(1.0), -lam)
-        probs = e * (weight / jnp.sum(e, axis=0, keepdims=True))
-        mix = (probs + pltpu.roll(probs, group_len, 1)).astype(jnp.bfloat16)
-        heads = dot(mix, v, TN)[:group_len]
-        inverse = lax.rsqrt(jnp.mean(heads * heads, axis=-1, keepdims=True) + EPSILON)
-        normed = heads * inverse
+        unweight = 1.0 / weight
         g = gain[:, at(c)]
-        result = (normed * g * active).astype(jnp.bfloat16)
-        if u < groups - 1:
-            att[tokens, at(c)] = result
-        else:
-            att_out[:, at(c)] = result
-        dn = upstream.astype(jnp.float32) * active * g
-        d_heads = (inverse * (dn - normed * jnp.mean(dn * normed, axis=-1, keepdims=True))).astype(jnp.bfloat16)
-        d_mix = dot(v, jnp.concatenate([d_heads, d_heads], axis=0), NT)
-        total = jnp.sum(d_mix * probs, axis=0, keepdims=True) * (1.0 / weight)
-        d_scores = (scale * probs * (d_mix - total)).astype(jnp.bfloat16)
-        blank = jnp.zeros_like(q2)
-        other = jnp.concatenate([d_heads, jnp.zeros_like(d_heads)], axis=0)
-        right_side = jnp.concatenate(
-            [jnp.concatenate([q2, blank], axis=1), jnp.concatenate([blank, other], axis=1)], axis=0
-        )
-        d_kv[here, :] = dot(jnp.concatenate([d_scores, mix], axis=1), right_side).astype(jnp.bfloat16)
+        blank = jnp.zeros((2 * group_len, cols), jnp.bfloat16)
+        blank_half = jnp.zeros((group_len, cols), jnp.bfloat16)
+        here = [slice(u * rows, (u + 1) * rows) for u in slots]
+        tokens = [slice((u + 1) * group_len, (u + 2) * group_len) for u in slots]
+        active = [jnp.clip(counts[0] - (seq * groups + u + 1), 0, 1).astype(jnp.float32) for u in slots]
+        count = range(len(slots))
+
+        def of_tokens(kind, i):
+            if slots[i] < groups - 1:
+                return qd[kind, tokens[i], at(c)]
+            return edge[kind, :, at(c)]
+
+        q2, scores = [], []
+        for i in count:
+            query = of_tokens(0, i)
+            zero = jnp.zeros_like(query)
+            q2.append(jnp.concatenate([jnp.where(on_first, query, zero), jnp.where(on_first, zero, query)], axis=0))
+        for i in count:
+            scores.append(dot(key[here[i], :], jnp.concatenate([q2[i], q2[i]], axis=1), NT) * scale)
+        e = [jnp.exp(scores[i] - jnp.max(scores[i], axis=0, keepdims=True)) for i in count]
+        probs = [e[i] * (weight / jnp.sum(e[i], axis=0, keepdims=True)) for i in count]
+        mix = [(probs[i] + pltpu.roll(probs[i], group_len, 1)).astype(jnp.bfloat16) for i in count]
+        heads = [dot(mix[i], value[here[i], :], TN)[:group_len] for i in count]
+        inverse = [lax.rsqrt(jnp.mean(heads[i] * heads[i], axis=-1, keepdims=True) + EPSILON) for i in count]
+        normed = [heads[i] * inverse[i] for i in count]
+        dn = [of_tokens(1, i).astype(jnp.float32) * active[i] * g for i in count]
+        d_heads = [
+            (inverse[i] * (dn[i] - normed[i] * jnp.mean(dn[i] * normed[i], axis=-1, keepdims=True))).astype(
+                jnp.bfloat16
+            )
+            for i in count
+        ]
+        d_mix = [dot(value[here[i], :], jnp.concatenate([d_heads[i], d_heads[i]], axis=0), NT) for i in count]
+        for i in count:
+            result = (normed[i] * g * active[i]).astype(jnp.bfloat16)
+            if slots[i] < groups - 1:
+                att[tokens[i], at(c)] = result
+            else:
+                att_out[:, at(c)] = result
+        total = [jnp.sum(d_mix[i] * probs[i], axis=0, keepdims=True) * unweight for i in count]
+        d_scores = [(scale * probs[i] * (d_mix[i] - total[i])).astype(jnp.bfloat16) for i in count]
+        for i in count:
+            other = jnp.concatenate([d_heads[i], blank_half], axis=0)
+            right_side = jnp.concatenate(
+                [jnp.concatenate([q2[i], blank], axis=1), jnp.concatenate([blank, other], axis=1)], axis=0
+            )
+            d_kv[here[i], :] = dot(jnp.concatenate([d_scores[i], mix[i]], axis=1), right_side).astype(jnp.bfloat16)
 
     def weight_part(c, core):
         part = w[c, pl.ds(core * grp_half, grp_half)]
@@ -267,28 +297,30 @@
     def step(c, first=False, final=False):
         if not final:
 
-            @pl.when(c + 2 < chunks)
+            @pl.when(c + 1 < by_grp)
             def _():
-                start_seq(c + 2)
-                start_edge(c + 2)
+                start_relay(c + 1)
+
+            @pl.when(c + 3 < by_grp)
+            def _():
+                start_seq(c + 3)
 
             @pl.when(c + 3 < chunks)
             def _():
-                start_grp(c + 3)
-
-        arrived(c)
-        project(c)
-        if not final:
-            start_relay(c + 1)
+                start_edge(c + 3)
+
         if not first:
-            gradients(c - 1)
 
             @pl.when(seq < n_seq - 1)
             def _():
                 edge_out(c - 1).start()
 
-        for u in range(groups):
-            attend(c, u)
+        arrived(c, final and by_grp < chunks)
+        project(c)
+        if not first:
+            gradients(c - 1)
+        for u in range(0, groups, TOGETHER):
+            attend(c, list(range(u, min(u + TOGETHER, groups))))
 
     step(0, first=True)
 
@@ -336,10 +368,25 @@
             total += got[o - 1, i].astype(jnp.float32)
         d_out[span, :] = total
 
+    def sent(copies):
+        for copy in copies:
+            copy.wait_send()
+
+    for c in range(by_grp, chunks):
+        sent(over_grp(c, True))
+        sent(over_seq(c, 0))
+        sent(relay(c, grp))
+
+    def drain_own(c, carry):
+        sent(over_grp(c))
+        for o in range(n_grp):
+            sent(over_seq(c, o))
+        sent(relay(c))
+        return carry
+
+    lax.fori_loop(0, by_grp, drain_own, 0)
+
     def drain(c, carry):
-        for copy in over_grp(c) + over_seq(c) + relay(c):
-            copy.wait_send()
-
         @pl.when(seq > 0)
         def _():
             edge_in(c).wait_send()
@@ -382,9 +429,9 @@
     bf16, f32 = jnp.bfloat16, jnp.float32
     vmem = pl.BlockSpec(memory_space=pltpu.VMEM)
     smem = pl.BlockSpec(memory_space=pltpu.SMEM)
-    hbm = pl.BlockSpec(memory_space=pl.ANY)
+    hbm = pl.BlockSpec(memory_space=pltpu.HBM)
     dma = pltpu.SemaphoreType.DMA
-    hops = max(2, w_seq)
+    ways = max(2, w_seq)
     att, d_neigh = pl.pallas_call(
         functools.partial(kernel, (n_grp, n_seq, n_mp, w_seq, chunks)),
         out_shape=(
@@ -410,8 +457,8 @@
             dma((chunks, 2)),
             dma((chunks, n_grp)),
             dma((chunks, n_grp)),
-            dma((chunks, hops)),
-            dma((chunks, hops)),
+            dma((chunks, ways, n_grp)),
+            dma((chunks, ways, n_grp)),
             dma((chunks, 2)),
             dma((chunks, 2)),
             dma((chunks,)),
@@ -422,7 +469,7 @@
             dma((n_mp, pieces)),
         ],
         compiler_params=pltpu.CompilerParams(
-            collective_id=0, has_side_effects=True, vmem_limit_bytes=48 * 1024 * 1024
+            collective_id=0, has_side_effects=True, vmem_limit_bytes=64400000
         ),
     )(lambdas, counts, queries[0], neighbours[0], w_key, w_value, gain.reshape(1, -1), d_out[0])
     att, d_neigh = pl.pallas_call(

time: 83.7 us -> 62.7 us (0.75)
  Pallas kernels: 75.2 us -> 61.2 us
  local copies, waits for them, and re-layouts: 6.81 us -> 0 us
    pallas_call x1, Pallas kernels: 73.7 us -> 59.7 us  [on_device(): pl.pallas_call(functools.partial(kernel, (n_grp, n_seq, n_mp, w_seq, chun...]
    unnamed x14 -> x0, local copies, waits for them, and re-layouts: 6.81 us -> none
where the time goes in v2:
time: 62.7 us; the launch traced here: 62.5 us
  Pallas kernels  61.2 us (98%)
  between operations  1.29 us (2%)
    pallas_call x1, Pallas kernels, on_device(): pl.pallas_call(functools.partial(kernel, (n_grp, n_seq, n_mp, w_seq, chun...  59.7 us
    pallas_call x1, Pallas kernels, on_device(): pl.pallas_call(put_out, out_shape=(jax.ShapeDtypeStruct((tokens, width),...  1.5 us

profile of v2, /device:TPU:0, one launch (start us, length us, event | category | flops | bytes accessed | tf_op | source)
XLA Modules:
  0.0 62.5 jit_solution(9035920536496763069)
XLA Ops:
  1.3 59.7 %shard_map.95 = (bf16[256,1024]{1,0:T(8,128)(2,1)S(1)}, f32[1024,512]{1,0:T(8,128)S(1)}) custom-call(f32[8]{0:T(128)} %lambdas.1, s32[1]{0:T(128)S(6)} %copy.10.counts, bf16[256,1024]{1,0:T(8,128)(2,1)} %bitcast.7, bf16[4,256,1024]{2,1,0:T(8,128)(2,1)} %bitcast.6, bf16[64,1024]{1,0:T(8,128)(2,1)} %wk_hbm.1, bf16[64,1024]{1,0:T(8,128)(2,1)} %wv_hbm.1, ...), custom_call_target="tpu_custom_call" | custom-call | tf_op jit(solution)/shard_map/pallas_call | solution.py:435
  61.0 1.5 %shard_map.96 = (bf16[256,1024]{1,0:T(8,128)(2,1)}, f32[1024,512]{1,0:T(8,128)}) custom-call(bf16[256,1024]{1,0:T(8,128)(2,1)S(1)} %get-tuple-element.6.att, f32[1024,512]{1,0:T(8,128)S(1)} %get-tuple-element.7.d_neigh), custom_call_target="tpu_custom_call" | custom-call | tf_op jit(solution)/shard_map/pallas_call | solution.py:475

commit v3 on v2

--- a/solution.py
+++ b/solution.py
@@ -20,16 +20,19 @@
 
 def kernel(
     sizes,
-    lambdas,
-    counts,
+    lambdas_hbm,
+    counts_hbm,
     q_hbm,
     n_hbm,
     wk_hbm,
     wv_hbm,
-    gain,
+    gain_hbm,
     do_hbm,
     att,
     d_out,
+    lambdas,
+    counts,
+    gain,
     x,
     qd,
     edge,
@@ -46,6 +49,8 @@
     own_sem,
     z_send,
     z_recv,
+    l_send,
+    l_recv,
     s_send,
     s_recv,
     r_send,
@@ -91,6 +96,9 @@
         pltpu.make_async_copy(q_hbm, qd.at[0], local_sem.at[0]),
         pltpu.make_async_copy(do_hbm, qd.at[1], local_sem.at[1]),
         pltpu.make_async_copy(n_hbm, x, local_sem.at[2]),
+        pltpu.make_async_copy(lambdas_hbm, lambdas, local_sem.at[3]),
+        pltpu.make_async_copy(counts_hbm, counts, local_sem.at[4]),
+        pltpu.make_async_copy(gain_hbm, gain, local_sem.at[5]),
     ]
     for copy in local:
         copy.start()
@@ -113,13 +121,49 @@
     else:
         targets = [lax.rem(seq + o, n_seq) for o in range(1, w_seq)]
     hops = range(1, n_grp)
-    by_grp = chunks - 1 if ring and chunks > 4 else chunks
-
-    def over_grp(c, whole=False):
-        block = w.at[c, grp] if whole else w.at[c, grp, w_pos]
+    by_seq = 2 if ring and chunks >= 8 and n_grp <= 4 else 0
+    by_grp = chunks - by_seq
+    seq_first = range(by_grp - 1, chunks - 1) if by_seq else range(0)
+
+    def nth(a):
+        if not by_seq:
+            return a
+        if isinstance(a, int):
+            return chunks - 1 if a == by_grp - 1 else a
+        return jnp.where(a == by_grp - 1, chunks - 1, a)
+
+    def over_grp(c):
+        block = w.at[c, grp, w_pos]
         return [
             remote(block, block, z_send.at[c, o], z_recv.at[c, o], {"grp": lax.rem(grp + o, n_grp)}) for o in hops
         ]
+
+    def line(c, k):
+        ways = []
+        for i, sign in enumerate((1, -1)):
+            source, target = grp - sign * k, grp + sign
+            block = w.at[c, jnp.clip(source, 0, n_grp - 1)]
+            copy = remote(
+                block,
+                block,
+                l_send.at[c, i, k],
+                l_recv.at[c, i, k],
+                {"grp": jnp.where(target < 0, 1, jnp.where(target >= n_grp, n_grp - 2, target))},
+            )
+            sends = (source >= 0) & (source < n_grp) & (target >= 0) & (target < n_grp)
+            arrives = (source - sign >= 0) & (source - sign < n_grp)
+            ways.append((copy, sends, arrives))
+        return ways
+
+    def start_line(c, k):
+        if k:
+            line_received(c, k - 1)
+        for copy, sends, _ in line(c, k):
+            pl.when(sends)(copy.start)
+
+    def line_received(c, k):
+        for copy, _, arrives in line(c, k):
+            pl.when(arrives)(copy.wait_recv)
 
     def over_seq(c, o):
         block = w.at[c, lax.rem(grp + n_grp - o, n_grp), w_pos]
@@ -174,20 +218,33 @@
         def _():
             edge_in(c).start()
 
-    def arrived(c, whole=False):
-        if whole:
-            received(over_grp(c, True))
+    def arrived(c, final):
+        if not by_seq or final or isinstance(c, int):
+            received(relay(c))
         else:
-            received(relay(c))
+
+            @pl.when(c < by_grp - 1)
+            def _():
+                received(relay(c))
+
+            @pl.when(c >= by_grp - 1)
+            def _():
+                line_received(c, n_grp - 2)
 
         @pl.when(seq < n_seq - 1)
         def _():
             edge_in(c).wait_recv()
 
-    for c in [*range(by_grp, chunks), *range(by_grp)]:
+    for c in seq_first:
         for copy in own(c):
             copy.wait()
-        if c < by_grp:
+        start(over_seq(c, 0))
+    soon = min(4, by_grp)
+    for a in range(by_grp):
+        c = nth(a)
+        for copy in own(c):
+            copy.wait()
+        if a < soon:
             start(over_grp(c))
         start(over_seq(c, 0))
     for copy in local[:2]:
@@ -204,19 +261,22 @@
         att_in[...] = jnp.zeros_like(att_in)
 
     acc[...] = jnp.zeros_like(acc)
-    for c in range(by_grp, chunks):
+    for c in seq_first:
         received(over_seq(c, 0))
         start(relay(c, grp))
     start_seq(0)
-    for c in range(by_grp, chunks):
+    for c in seq_first:
         received(relay(c, grp))
-        start(over_grp(c, True))
+        start_line(c, 0)
+    for a in range(soon, by_grp):
+        start(over_grp(nth(a)))
     if by_grp > 1:
         start_seq(1)
     start_relay(0)
     if by_grp > 2:
         start_seq(2)
-    local[2].wait()
+    for copy in local[2:]:
+        copy.wait()
 
     scale = head_dim ** (-0.5)
     lane = lax.broadcasted_iota(jnp.int32, (group_len, cols), 1)
@@ -299,11 +359,19 @@
 
             @pl.when(c + 1 < by_grp)
             def _():
-                start_relay(c + 1)
+                start_relay(nth(c + 1))
 
             @pl.when(c + 3 < by_grp)
             def _():
-                start_seq(c + 3)
+                start_seq(nth(c + 3))
+
+            if by_seq and not first:
+                for k in range(1, n_grp - 1):
+
+                    @pl.when(c == 2 * k - 1)
+                    def _(k=k):
+                        for b in seq_first:
+                            start_line(b, k)
 
             @pl.when(c + 3 < chunks)
             def _():
@@ -315,7 +383,7 @@
             def _():
                 edge_out(c - 1).start()
 
-        arrived(c, final and by_grp < chunks)
+        arrived(c, final)
         project(c)
         if not first:
             gradients(c - 1)
@@ -372,12 +440,15 @@
         for copy in copies:
             copy.wait_send()
 
-    for c in range(by_grp, chunks):
-        sent(over_grp(c, True))
+    for c in seq_first:
         sent(over_seq(c, 0))
         sent(relay(c, grp))
-
-    def drain_own(c, carry):
+        for k in range(n_grp - 1):
+            for copy, sends, _ in line(c, k):
+                pl.when(sends)(copy.wait_send)
+
+    def drain_own(a, carry):
+        c = nth(a)
         sent(over_grp(c))
         for o in range(n_grp):
             sent(over_seq(c, o))
@@ -428,7 +499,6 @@
     pieces = 2
     bf16, f32 = jnp.bfloat16, jnp.float32
     vmem = pl.BlockSpec(memory_space=pltpu.VMEM)
-    smem = pl.BlockSpec(memory_space=pltpu.SMEM)
     hbm = pl.BlockSpec(memory_space=pltpu.HBM)
     dma = pltpu.SemaphoreType.DMA
     ways = max(2, w_seq)
@@ -438,9 +508,12 @@
             pltpu.VMEM((tokens, width), bf16),
             pltpu.VMEM((groups * rows, half), f32),
         ),
-        in_specs=[smem, smem, hbm, hbm, hbm, hbm, vmem, hbm],
+        in_specs=[hbm] * 8,
         out_specs=(vmem, vmem),
         scratch_shapes=[
+            pltpu.SMEM((chunks,), f32),
+            pltpu.SMEM((1,), jnp.int32),
+            pltpu.VMEM((1, width), f32),
             pltpu.VMEM((groups, rows, enc), bf16),
             pltpu.VMEM((2, tokens, width), bf16),
             pltpu.VMEM((2, group_len, width), bf16),
@@ -453,10 +526,12 @@
             pltpu.VMEM((group_len, width), bf16),
             pltpu.VMEM((n_mp - 1, pieces, groups * rows // pieces, half), bf16),
             pltpu.VMEM((n_mp - 1, pieces, groups * rows // pieces, half), bf16),
-            dma((3,)),
+            dma((6,)),
             dma((chunks, 2)),
             dma((chunks, n_grp)),
             dma((chunks, n_grp)),
+            dma((chunks, 2, n_grp)),
+            dma((chunks, 2, n_grp)),
             dma((chunks, ways, n_grp)),
             dma((chunks, ways, n_grp)),
             dma((chunks, 2)),

time: 62.7 us -> 60.4 us (0.963)
  Pallas kernels: 61.2 us -> 58.9 us
    pallas_call x1, Pallas kernels: 59.7 us -> 57.4 us  [on_device(): pl.pallas_call(functools.partial(kernel, (n_grp, n_seq, n_mp, w_seq, chun...]
where the time goes in v3:
time: 60.4 us; the launch traced here: 60.2 us
  Pallas kernels  58.9 us (98%)
  between operations  1.29 us (2%)
    pallas_call x1, Pallas kernels, on_device(): pl.pallas_call(functools.partial(kernel, (n_grp, n_seq, n_mp, w_seq, chun...  57.4 us
    pallas_call x1, Pallas kernels, on_device(): pl.pallas_call(put_out, out_shape=(jax.ShapeDtypeStruct((tokens, width),...  1.5 us

profile of v3, /device:TPU:0, one launch (start us, length us, event | category | flops | bytes accessed | tf_op | source)
XLA Modules:
  0.0 60.2 jit_solution(12806320016433421096)
XLA Ops:
  1.3 57.4 %shard_map.95 = (bf16[256,1024]{1,0:T(8,128)(2,1)S(1)}, f32[1024,512]{1,0:T(8,128)S(1)}) custom-call(f32[8]{0:T(128)} %lambdas_hbm.1, s32[1]{0:T(128)S(6)} %copy.10.counts_hbm, bf16[256,1024]{1,0:T(8,128)(2,1)} %bitcast.7, bf16[4,256,1024]{2,1,0:T(8,128)(2,1)} %bitcast.6, bf16[64,1024]{1,0:T(8,128)(2,1)} %wk_hbm.1, bf16[64,1024]{1,0:T(8,128)(2,1)} %wv_hbm.1, ...), custom_call_target="tpu_custom_call" | custom-call | tf_op jit(solution)/shard_map/pallas_call | solution.py:505
  58.7 1.5 %shard_map.96 = (bf16[256,1024]{1,0:T(8,128)(2,1)}, f32[1024,512]{1,0:T(8,128)}) custom-call(bf16[256,1024]{1,0:T(8,128)(2,1)S(1)} %get-tuple-element.6.att, f32[1024,512]{1,0:T(8,128)S(1)} %get-tuple-element.7.d_neigh), custom_call_target="tpu_custom_call" | custom-call | tf_op jit(solution)/shard_map/pallas_call | solution.py:550

commit v4 on v3

--- a/solution.py
+++ b/solution.py
@@ -84,10 +84,14 @@
     def own(c):
         return [
             pltpu.make_async_copy(
-                src.at[:, at(c)], w.at[c, grp, w_pos, :, pl.ds(kind * cols, cols)], own_sem.at[c, kind]
+                src.at[:, at(c)], w.at[c, grp, w_pos, :, pl.ds(kind * cols, cols)], own_sem.at[c]
             )
             for kind, src in enumerate((wk_hbm, wv_hbm))
         ]
+
+    def own_arrived(c):
+        block = w.at[c, grp, w_pos]
+        pltpu.make_async_copy(block, block, own_sem.at[c]).wait()
 
     for c in range(chunks):
         for copy in own(c):
@@ -123,31 +127,35 @@
     hops = range(1, n_grp)
     by_seq = 2 if ring and chunks >= 8 and n_grp <= 4 else 0
     by_grp = chunks - by_seq
-    seq_first = range(by_grp - 1, chunks - 1) if by_seq else range(0)
+    seq_first = (chunks - 4, chunks - 2) if by_seq else ()
+    plain = by_grp - 2 if by_seq else by_grp
 
     def nth(a):
-        if not by_seq:
-            return a
+        late = 2 * a - plain + 1
         if isinstance(a, int):
-            return chunks - 1 if a == by_grp - 1 else a
-        return jnp.where(a == by_grp - 1, chunks - 1, a)
+            return a if a < plain else late
+        return jnp.where(a < plain, a, late)
+
+    def bulk(block, send_sem, recv_sem):
+        return remote(block, block, send_sem, recv_sem, {"grp": lax.rem(grp + 1, n_grp)})
 
     def over_grp(c):
         block = w.at[c, grp, w_pos]
         return [
-            remote(block, block, z_send.at[c, o], z_recv.at[c, o], {"grp": lax.rem(grp + o, n_grp)}) for o in hops
+            remote(block, block, z_send.at[c], z_recv.at[c, o - 1], {"grp": lax.rem(grp + o, n_grp)}) for o in hops
         ]
 
     def line(c, k):
         ways = []
+        b = (c - seq_first[0]) // (seq_first[1] - seq_first[0])
         for i, sign in enumerate((1, -1)):
             source, target = grp - sign * k, grp + sign
             block = w.at[c, jnp.clip(source, 0, n_grp - 1)]
             copy = remote(
                 block,
                 block,
-                l_send.at[c, i, k],
-                l_recv.at[c, i, k],
+                l_send.at[b, i, k],
+                l_recv.at[b, i, k],
                 {"grp": jnp.where(target < 0, 1, jnp.where(target >= n_grp, n_grp - 2, target))},
             )
             sends = (source >= 0) & (source < n_grp) & (target >= 0) & (target < n_grp)
@@ -168,9 +176,11 @@
     def over_seq(c, o):
         block = w.at[c, lax.rem(grp + n_grp - o, n_grp), w_pos]
         return [
-            remote(block, block, s_send.at[c, i, o], s_recv.at[c, i, o], {"seq": target})
-            for i, target in enumerate(targets)
+            remote(block, block, s_send.at[c], s_recv.at[c], {"seq": target}) for target in targets
         ]
+
+    def all_seq(c, grps=slice(None)):
+        return [bulk(w.at[c, grps, pl.ds(0, len(targets))], s_send.at[c], s_recv.at[c])] if targets else []
 
     def relay(c, grps=slice(None)):
         if not ring:
@@ -178,21 +188,24 @@
         copies = []
         for i, (source, target) in enumerate(((left, right), (right, left))):
             passed = w.at[c, grps, source, :, pl.ds(i * cols, cols)]
-            copies.append(remote(passed, passed, r_send.at[c, i], r_recv.at[c, i], {"seq": target}))
+            copies.append(remote(passed, passed, r_send.at[c], r_recv.at[c], {"seq": target}))
         return copies
+
+    def all_relay(c, grps=slice(None)):
+        return [bulk(w.at[c, grps, 0], r_send.at[c], r_recv.at[c])] if ring else []
 
     def edge_in(c):
         return remote(
             qd.at[:, pl.ds(0, group_len), at(c)],
             edge.at[:, :, at(c)],
-            e_send.at[c],
+            e_send.at[0],
             e_recv.at[c],
             {"seq": preceding},
         )
 
     def edge_out(c):
         return remote(
-            att_out.at[:, at(c)], att_in.at[:, at(c)], a_send.at[c], a_recv.at[c], {"seq": following}
+            att_out.at[:, at(c)], att_in.at[:, at(c)], a_send.at[0], a_recv.at[0], {"seq": following}
         )
 
     def start(copies):
@@ -209,8 +222,7 @@
             start(over_seq(c, o))
 
     def start_relay(c):
-        for o in range(n_grp):
-            received(over_seq(c, o))
+        received(all_seq(c))
         start(relay(c))
 
     def start_edge(c):
@@ -218,16 +230,19 @@
         def _():
             edge_in(c).start()
 
-    def arrived(c, final):
-        if not by_seq or final or isinstance(c, int):
-            received(relay(c))
+    def arrived(c):
+        if isinstance(c, int):
+            received(all_relay(c))
+        elif not by_seq:
+            received(all_relay(c))
         else:
-
-            @pl.when(c < by_grp - 1)
+            lined = (c == seq_first[0]) | (c == seq_first[1])
+
+            @pl.when(jnp.logical_not(lined))
             def _():
-                received(relay(c))
-
-            @pl.when(c >= by_grp - 1)
+                received(all_relay(c))
+
+            @pl.when(lined)
             def _():
                 line_received(c, n_grp - 2)
 
@@ -235,22 +250,24 @@
         def _():
             edge_in(c).wait_recv()
 
+    def own_seq(a):
+        if a < by_grp:
+            start(over_seq(nth(a), 0))
+
+    def own_grp(a):
+        own_arrived(nth(a))
+        start(over_grp(nth(a)))
+
     for c in seq_first:
-        for copy in own(c):
-            copy.wait()
+        own_arrived(c)
         start(over_seq(c, 0))
-    soon = min(4, by_grp)
-    for a in range(by_grp):
-        c = nth(a)
-        for copy in own(c):
-            copy.wait()
-        if a < soon:
-            start(over_grp(c))
-        start(over_seq(c, 0))
+    own_grp(0)
+    own_seq(0)
+    for a in range(1, min(4, by_grp)):
+        own_grp(a)
+    own_seq(1)
     for copy in local[:2]:
         copy.wait()
-    for c in range(min(3, chunks)):
-        start_edge(c)
 
     @pl.when(seq == n_seq - 1)
     def _():
@@ -262,23 +279,34 @@
 
     acc[...] = jnp.zeros_like(acc)
     for c in seq_first:
-        received(over_seq(c, 0))
+        received(all_seq(c, 0))
         start(relay(c, grp))
+    start_edge(0)
+    if chunks > 1:
+        start_edge(1)
+    own_seq(2)
     start_seq(0)
+    own_seq(3)
     for c in seq_first:
-        received(relay(c, grp))
+        received(all_relay(c, 0))
         start_line(c, 0)
-    for a in range(soon, by_grp):
-        start(over_grp(nth(a)))
+    for a in range(4, by_grp):
+        own_grp(a)
     if by_grp > 1:
         start_seq(1)
     start_relay(0)
+    if chunks > 2:
+        start_edge(2)
+    own_seq(4)
     if by_grp > 2:
         start_seq(2)
+    for a in range(5, by_grp):
+        own_seq(a)
     for copy in local[2:]:
         copy.wait()
 
     scale = head_dim ** (-0.5)
+    folded = scale.hex().startswith("0x1.0000000000000p")
     lane = lax.broadcasted_iota(jnp.int32, (group_len, cols), 1)
     on_first = lane < head_dim
     lane_row = lax.broadcasted_iota(jnp.int32, (1, 2 * group_len), 1)
@@ -313,10 +341,14 @@
         q2, scores = [], []
         for i in count:
             query = of_tokens(0, i)
+            if folded:
+                query = (query.astype(jnp.float32) * scale).astype(jnp.bfloat16)
             zero = jnp.zeros_like(query)
             q2.append(jnp.concatenate([jnp.where(on_first, query, zero), jnp.where(on_first, zero, query)], axis=0))
         for i in count:
-            scores.append(dot(key[here[i], :], jnp.concatenate([q2[i], q2[i]], axis=1), NT) * scale)
+            scores.append(dot(key[here[i], :], jnp.concatenate([q2[i], q2[i]], axis=1), NT))
+            if not folded:
+                scores[i] = scores[i] * scale
         e = [jnp.exp(scores[i] - jnp.max(scores[i], axis=0, keepdims=True)) for i in count]
         probs = [e[i] * (weight / jnp.sum(e[i], axis=0, keepdims=True)) for i in count]
         mix = [(probs[i] + pltpu.roll(probs[i], group_len, 1)).astype(jnp.bfloat16) for i in count]
@@ -338,13 +370,11 @@
             else:
                 att_out[:, at(c)] = result
         total = [jnp.sum(d_mix[i] * probs[i], axis=0, keepdims=True) * unweight for i in count]
-        d_scores = [(scale * probs[i] * (d_mix[i] - total[i])).astype(jnp.bfloat16) for i in count]
+        outer = probs if folded else [scale * probs[i] for i in count]
+        d_scores = [(outer[i] * (d_mix[i] - total[i])).astype(jnp.bfloat16) for i in count]
         for i in count:
-            other = jnp.concatenate([d_heads[i], blank_half], axis=0)
-            right_side = jnp.concatenate(
-                [jnp.concatenate([q2[i], blank], axis=1), jnp.concatenate([blank, other], axis=1)], axis=0
-            )
-            d_kv[here[i], :] = dot(jnp.concatenate([d_scores[i], mix[i]], axis=1), right_side).astype(jnp.bfloat16)
+            d_kv[here[i], :cols] = dot(d_scores[i], q2[i]).astype(jnp.bfloat16)
+            d_kv[here[i], cols:] = dot(mix[i], jnp.concatenate([d_heads[i], blank_half], axis=0)).astype(jnp.bfloat16)
 
     def weight_part(c, core):
         part = w[c, pl.ds(core * grp_half, grp_half)]
@@ -354,24 +384,29 @@
         for core in range(n_mp):
             acc[core] += dot(d_kv[...], weight_part(c, core), NT)
 
+    def lines(c, i):
+        for k in range(1, n_grp - 1):
+
+            @pl.when(c == 2 * k - 1)
+            def _(k=k):
+                start_line(seq_first[i], k)
+
     def step(c, first=False, final=False):
         if not final:
 
-            @pl.when(c + 1 < by_grp)
+            @pl.when(c + 1 < min(plain + 1, by_grp))
             def _():
                 start_relay(nth(c + 1))
 
-            @pl.when(c + 3 < by_grp)
+            @pl.when(c + 3 < plain)
             def _():
                 start_seq(nth(c + 3))
 
-            if by_seq and not first:
-                for k in range(1, n_grp - 1):
-
-                    @pl.when(c == 2 * k - 1)
-                    def _(k=k):
-                        for b in seq_first:
-                            start_line(b, k)
+            if not first:
+
+                @pl.when((c + 2 >= plain) & (c + 2 < by_grp))
+                def _():
+                    start_seq(nth(c + 2))
 
             @pl.when(c + 3 < chunks)
             def _():
@@ -383,10 +418,19 @@
             def _():
                 edge_out(c - 1).start()
 
-        arrived(c, final)
+        if by_seq and not first and not final:
+            lines(c, 0)
+        arrived(c)
         project(c)
         if not first:
             gradients(c - 1)
+        if by_seq and not first and not final:
+            lines(c, 1)
+
+            @pl.when(c == plain)
+            def _():
+                start_relay(nth(plain + 1))
+
         for u in range(0, groups, TOGETHER):
             attend(c, list(range(u, min(u + TOGETHER, groups))))
 
@@ -405,7 +449,7 @@
 
     def exchange(o, i):
         return remote(
-            send.at[o - 1, i], got.at[o - 1, i], g_send.at[o, i], g_recv.at[o, i], {"mp": lax.rem(mp + o, n_mp)}
+            send.at[o - 1, i], got.at[o - 1, i], g_send.at[o - 1, i], g_recv.at[o - 1, i], {"mp": lax.rem(mp + o, n_mp)}
         )
 
     for o in range(1, n_mp):
@@ -424,8 +468,7 @@
 
     @pl.when(seq > 0)
     def _():
-        for c in range(chunks):
-            edge_out(c).wait_recv()
+        bulk(att_in, a_send.at[0], a_recv.at[0]).wait_recv()
 
     att[:group_len, :] = att_in[...]
     for i in range(pieces):
@@ -441,34 +484,25 @@
             copy.wait_send()
 
     for c in seq_first:
-        sent(over_seq(c, 0))
-        sent(relay(c, grp))
+        sent(all_seq(c, 0))
+        sent(all_relay(c, 0))
         for k in range(n_grp - 1):
             for copy, sends, _ in line(c, k):
                 pl.when(sends)(copy.wait_send)
 
-    def drain_own(a, carry):
+    for a in range(by_grp):
         c = nth(a)
-        sent(over_grp(c))
-        for o in range(n_grp):
-            sent(over_seq(c, o))
-        sent(relay(c))
-        return carry
-
-    lax.fori_loop(0, by_grp, drain_own, 0)
-
-    def drain(c, carry):
-        @pl.when(seq > 0)
-        def _():
-            edge_in(c).wait_send()
-
-        @pl.when(seq < n_seq - 1)
-        def _():
-            edge_out(c).wait_send()
-
-        return carry
-
-    lax.fori_loop(0, chunks, drain, 0)
+        bulk(w.at[c, pl.ds(0, n_grp - 1), w_pos], z_send.at[c], z_recv.at[c, 0]).wait_send()
+        sent(all_seq(c))
+        sent(all_relay(c))
+
+    @pl.when(seq > 0)
+    def _():
+        bulk(edge, e_send.at[0], e_recv.at[0]).wait_send()
+
+    @pl.when(seq < n_seq - 1)
+    def _():
+        bulk(att_in, a_send.at[0], a_recv.at[0]).wait_send()
 
 
 def put_out(att, d_neigh, att_hbm, d_hbm, sem):
@@ -501,7 +535,6 @@
     vmem = pl.BlockSpec(memory_space=pltpu.VMEM)
     hbm = pl.BlockSpec(memory_space=pltpu.HBM)
     dma = pltpu.SemaphoreType.DMA
-    ways = max(2, w_seq)
     att, d_neigh = pl.pallas_call(
         functools.partial(kernel, (n_grp, n_seq, n_mp, w_seq, chunks)),
         out_shape=(
@@ -527,21 +560,21 @@
             pltpu.VMEM((n_mp - 1, pieces, groups * rows // pieces, half), bf16),
             pltpu.VMEM((n_mp - 1, pieces, groups * rows // pieces, half), bf16),
             dma((6,)),
-            dma((chunks, 2)),
-            dma((chunks, n_grp)),
-            dma((chunks, n_grp)),
-            dma((chunks, 2, n_grp)),
-            dma((chunks, 2, n_grp)),
-            dma((chunks, ways, n_grp)),
-            dma((chunks, ways, n_grp)),
-            dma((chunks, 2)),
-            dma((chunks, 2)),
+            dma((chunks,)),
+            dma((chunks,)),
+            dma((chunks, n_grp - 1)),
+            dma((2, 2, n_grp - 1)),
+            dma((2, 2, n_grp - 1)),
             dma((chunks,)),
             dma((chunks,)),
             dma((chunks,)),
             dma((chunks,)),
-            dma((n_mp, pieces)),
-            dma((n_mp, pieces)),
+            dma((1,)),
+            dma((chunks,)),
+            dma((1,)),
+            dma((1,)),
+            dma((n_mp - 1, pieces)),
+            dma((n_mp - 1, pieces)),
         ],
         compiler_params=pltpu.CompilerParams(
             collective_id=0, has_side_effects=True, vmem_limit_bytes=64400000

time: 60.4 us -> 55.7 us (0.922)
  Pallas kernels: 58.9 us -> 54.3 us
    pallas_call x1, Pallas kernels: 57.4 us -> 52.8 us  [on_device(): pl.pallas_call(functools.partial(kernel, (n_grp, n_seq, n_mp, w_seq, chun...]
where the time goes in v4:
time: 55.7 us; the launch traced here: 55.6 us
  Pallas kernels  54.3 us (97%)
  between operations  1.29 us (2%)
    pallas_call x1, Pallas kernels, on_device(): pl.pallas_call(functools.partial(kernel, (n_grp, n_seq, n_mp, w_seq, chun...  52.8 us
    pallas_call x1, Pallas kernels, on_device(): pl.pallas_call(put_out, out_shape=(jax.ShapeDtypeStruct((tokens, width),...  1.5 us

profile of v4, /device:TPU:0, one launch (start us, length us, event | category | flops | bytes accessed | tf_op | source)
XLA Modules:
  0.0 55.6 jit_solution(17432567383001028408)
XLA Ops:
  1.3 52.8 %shard_map.95 = (bf16[256,1024]{1,0:T(8,128)(2,1)S(1)}, f32[1024,512]{1,0:T(8,128)S(1)}) custom-call(f32[8]{0:T(128)} %lambdas_hbm.1, s32[1]{0:T(128)S(6)} %copy.10.counts_hbm, bf16[256,1024]{1,0:T(8,128)(2,1)} %bitcast.7, bf16[4,256,1024]{2,1,0:T(8,128)(2,1)} %bitcast.6, bf16[64,1024]{1,0:T(8,128)(2,1)} %wk_hbm.1, bf16[64,1024]{1,0:T(8,128)(2,1)} %wv_hbm.1, ...), custom_call_target="tpu_custom_call" | custom-call | tf_op jit(solution)/shard_map/pallas_call | solution.py:538
  54.1 1.5 %shard_map.96 = (bf16[256,1024]{1,0:T(8,128)(2,1)}, f32[1024,512]{1,0:T(8,128)}) custom-call(bf16[256,1024]{1,0:T(8,128)(2,1)S(1)} %get-tuple-element.6.att, f32[1024,512]{1,0:T(8,128)S(1)} %get-tuple-element.7.d_neigh), custom_call_target="tpu_custom_call" | custom-call | tf_op jit(solution)/shard_map/pallas_call | solution.py:583

commit v5 on v4

--- a/solution.py
+++ b/solution.py
@@ -84,14 +84,14 @@
     def own(c):
         return [
             pltpu.make_async_copy(
-                src.at[:, at(c)], w.at[c, grp, w_pos, :, pl.ds(kind * cols, cols)], own_sem.at[c]
+                src.at[:, at(c)], w.at[c, grp, w_pos, :, pl.ds(kind * cols, cols)], own_sem.at[0]
             )
             for kind, src in enumerate((wk_hbm, wv_hbm))
         ]
 
-    def own_arrived(c):
-        block = w.at[c, grp, w_pos]
-        pltpu.make_async_copy(block, block, own_sem.at[c]).wait()
+    def own_arrived():
+        block = w.at[:, grp, w_pos]
+        pltpu.make_async_copy(block, block, own_sem.at[0]).wait()
 
     for c in range(chunks):
         for copy in own(c):
@@ -136,13 +136,20 @@
             return a if a < plain else late
         return jnp.where(a < plain, a, late)
 
+    def group_of(c):
+        if not by_seq:
+            return 0
+        if isinstance(c, int):
+            return int(c in seq_first)
+        return ((c == seq_first[0]) | (c == seq_first[1])).astype(jnp.int32)
+
     def bulk(block, send_sem, recv_sem):
         return remote(block, block, send_sem, recv_sem, {"grp": lax.rem(grp + 1, n_grp)})
 
     def over_grp(c):
         block = w.at[c, grp, w_pos]
         return [
-            remote(block, block, z_send.at[c], z_recv.at[c, o - 1], {"grp": lax.rem(grp + o, n_grp)}) for o in hops
+            remote(block, block, z_send.at[0], z_recv.at[c, o - 1], {"grp": lax.rem(grp + o, n_grp)}) for o in hops
         ]
 
     def line(c, k):
@@ -176,11 +183,11 @@
     def over_seq(c, o):
         block = w.at[c, lax.rem(grp + n_grp - o, n_grp), w_pos]
         return [
-            remote(block, block, s_send.at[c], s_recv.at[c], {"seq": target}) for target in targets
+            remote(block, block, s_send.at[group_of(c)], s_recv.at[c], {"seq": target}) for target in targets
         ]
 
     def all_seq(c, grps=slice(None)):
-        return [bulk(w.at[c, grps, pl.ds(0, len(targets))], s_send.at[c], s_recv.at[c])] if targets else []
+        return [bulk(w.at[c, grps, pl.ds(0, len(targets))], s_send.at[group_of(c)], s_recv.at[c])] if targets else []
 
     def relay(c, grps=slice(None)):
         if not ring:
@@ -188,11 +195,11 @@
         copies = []
         for i, (source, target) in enumerate(((left, right), (right, left))):
             passed = w.at[c, grps, source, :, pl.ds(i * cols, cols)]
-            copies.append(remote(passed, passed, r_send.at[c], r_recv.at[c], {"seq": target}))
+            copies.append(remote(passed, passed, r_send.at[group_of(c)], r_recv.at[c], {"seq": target}))
         return copies
 
     def all_relay(c, grps=slice(None)):
-        return [bulk(w.at[c, grps, 0], r_send.at[c], r_recv.at[c])] if ring else []
+        return [bulk(w.at[c, grps, 0], r_send.at[group_of(c)], r_recv.at[c])] if ring else []
 
     def edge_in(c):
         return remote(
@@ -255,11 +262,10 @@
             start(over_seq(nth(a), 0))
 
     def own_grp(a):
-        own_arrived(nth(a))
         start(over_grp(nth(a)))
 
+    own_arrived()
     for c in seq_first:
-        own_arrived(c)
         start(over_seq(c, 0))
     own_grp(0)
     own_seq(0)
@@ -484,17 +490,18 @@
             copy.wait_send()
 
     for c in seq_first:
-        sent(all_seq(c, 0))
-        sent(all_relay(c, 0))
         for k in range(n_grp - 1):
             for copy, sends, _ in line(c, k):
                 pl.when(sends)(copy.wait_send)
-
-    for a in range(by_grp):
-        c = nth(a)
-        bulk(w.at[c, pl.ds(0, n_grp - 1), w_pos], z_send.at[c], z_recv.at[c, 0]).wait_send()
-        sent(all_seq(c))
-        sent(all_relay(c))
+    many = pl.ds(0, by_grp)
+    bulk(w.at[many, pl.ds(0, n_grp - 1), w_pos], z_send.at[0], z_recv.at[0, 0]).wait_send()
+    if targets:
+        bulk(w.at[many, :, pl.ds(0, len(targets))], s_send.at[0], s_recv.at[0]).wait_send()
+    if ring:
+        bulk(w.at[many, :, 0], r_send.at[0], r_recv.at[0]).wait_send()
+    if by_seq:
+        bulk(w.at[pl.ds(0, by_seq), 0, pl.ds(0, len(targets))], s_send.at[1], s_recv.at[0]).wait_send()
+        bulk(w.at[pl.ds(0, by_seq), 0, 0], r_send.at[1], r_recv.at[0]).wait_send()
 
     @pl.when(seq > 0)
     def _():
@@ -560,14 +567,14 @@
             pltpu.VMEM((n_mp - 1, pieces, groups * rows // pieces, half), bf16),
             pltpu.VMEM((n_mp - 1, pieces, groups * rows // pieces, half), bf16),
             dma((6,)),
-            dma((chunks,)),
-            dma((chunks,)),
+            dma((1,)),
+            dma((1,)),
             dma((chunks, n_grp - 1)),
             dma((2, 2, n_grp - 1)),
             dma((2, 2, n_grp - 1)),
+            dma((2,)),
             dma((chunks,)),
-            dma((chunks,)),
-            dma((chunks,)),
+            dma((2,)),
             dma((chunks,)),
             dma((1,)),
             dma((chunks,)),

time: 55.7 us -> 55.5 us (level)
  no operation moved by 1% of the time
where the time goes in v5:
time: 55.5 us; the launch traced here: 55.3 us
  Pallas kernels  54 us (97%)
  between operations  1.29 us (2%)
    pallas_call x1, Pallas kernels, on_device(): pl.pallas_call(functools.partial(kernel, (n_grp, n_seq, n_mp, w_seq, chun...  52.5 us
    pallas_call x1, Pallas kernels, on_device(): pl.pallas_call(put_out, out_shape=(jax.ShapeDtypeStruct((tokens, width),...  1.5 us

profile of v5, /device:TPU:0, one launch (start us, length us, event | category | flops | bytes accessed | tf_op | source)
XLA Modules:
  0.0 55.3 jit_solution(6829370370859055030)
XLA Ops:
  1.3 52.5 %shard_map.95 = (bf16[256,1024]{1,0:T(8,128)(2,1)S(1)}, f32[1024,512]{1,0:T(8,128)S(1)}) custom-call(f32[8]{0:T(128)} %lambdas_hbm.1, s32[1]{0:T(128)S(6)} %copy.10.counts_hbm, bf16[256,1024]{1,0:T(8,128)(2,1)} %bitcast.7, bf16[4,256,1024]{2,1,0:T(8,128)(2,1)} %bitcast.6, bf16[64,1024]{1,0:T(8,128)(2,1)} %wk_hbm.1, bf16[64,1024]{1,0:T(8,128)(2,1)} %wv_hbm.1, ...), custom_call_target="tpu_custom_call" | custom-call | tf_op jit(solution)/shard_map/pallas_call | solution.py:545
  53.8 1.5 %shard_map.96 = (bf16[256,1024]{1,0:T(8,128)(2,1)}, f32[1024,512]{1,0:T(8,128)}) custom-call(bf16[256,1024]{1,0:T(8,128)(2,1)S(1)} %get-tuple-element.6.att, f32[1024,512]{1,0:T(8,128)S(1)} %get-tuple-element.7.d_neigh), custom_call_target="tpu_custom_call" | custom-call | tf_op jit(solution)/shard_map/pallas_call | solution.py:590

commit v6 on v5

--- a/solution.py
+++ b/solution.py
@@ -143,13 +143,16 @@
             return int(c in seq_first)
         return ((c == seq_first[0]) | (c == seq_first[1])).astype(jnp.int32)
 
+    def grp_slot(c, o):
+        return c * (n_grp - 1) + o - 1 if isinstance(c, int) and c < 2 else c + 2 * (n_grp - 2)
+
     def bulk(block, send_sem, recv_sem):
         return remote(block, block, send_sem, recv_sem, {"grp": lax.rem(grp + 1, n_grp)})
 
     def over_grp(c):
         block = w.at[c, grp, w_pos]
         return [
-            remote(block, block, z_send.at[0], z_recv.at[c, o - 1], {"grp": lax.rem(grp + o, n_grp)}) for o in hops
+            remote(block, block, z_send.at[0], z_recv.at[grp_slot(c, o)], {"grp": lax.rem(grp + o, n_grp)}) for o in hops
         ]
 
     def line(c, k):
@@ -224,8 +227,12 @@
             copy.wait_recv()
 
     def start_seq(c):
+        fine = isinstance(c, int) and c < 2
+        if not fine:
+            bulk(w.at[c, pl.ds(0, n_grp - 1), w_pos], z_send.at[0], z_recv.at[grp_slot(c, 1)]).wait_recv()
         for o, arrival in zip(hops, over_grp(c)):
-            arrival.wait_recv()
+            if fine:
+                arrival.wait_recv()
             start(over_seq(c, o))
 
     def start_relay(c):
@@ -494,7 +501,7 @@
             for copy, sends, _ in line(c, k):
                 pl.when(sends)(copy.wait_send)
     many = pl.ds(0, by_grp)
-    bulk(w.at[many, pl.ds(0, n_grp - 1), w_pos], z_send.at[0], z_recv.at[0, 0]).wait_send()
+    bulk(w.at[many, pl.ds(0, n_grp - 1), w_pos], z_send.at[0], z_recv.at[0]).wait_send()
     if targets:
         bulk(w.at[many, :, pl.ds(0, len(targets))], s_send.at[0], s_recv.at[0]).wait_send()
     if ring:
@@ -569,7 +576,7 @@
             dma((6,)),
             dma((1,)),
             dma((1,)),
-            dma((chunks, n_grp - 1)),
+            dma((chunks + 2 * (n_grp - 2),)),
             dma((2, 2, n_grp - 1)),
             dma((2, 2, n_grp - 1)),
             dma((2,)),

time: 55.5 us -> 55.3 us (level)
  no operation moved by 1% of the time
where the time goes in v6:
time: 55.3 us; the launch traced here: 55.2 us
  Pallas kernels  53.9 us (97%)
  between operations  1.29 us (2%)
    pallas_call x1, Pallas kernels, on_device(): pl.pallas_call(functools.partial(kernel, (n_grp, n_seq, n_mp, w_seq, chun...  52.4 us
    pallas_call x1, Pallas kernels, on_device(): pl.pallas_call(put_out, out_shape=(jax.ShapeDtypeStruct((tokens, width),...  1.5 us

profile of v6, /device:TPU:0, one launch (start us, length us, event | category | flops | bytes accessed | tf_op | source)
XLA Modules:
  0.0 55.2 jit_solution(18220219647116793638)
XLA Ops:
  1.3 52.4 %shard_map.95 = (bf16[256,1024]{1,0:T(8,128)(2,1)S(1)}, f32[1024,512]{1,0:T(8,128)S(1)}) custom-call(f32[8]{0:T(128)} %lambdas_hbm.1, s32[1]{0:T(128)S(6)} %copy.10.counts_hbm, bf16[256,1024]{1,0:T(8,128)(2,1)} %bitcast.7, bf16[4,256,1024]{2,1,0:T(8,128)(2,1)} %bitcast.6, bf16[64,1024]{1,0:T(8,128)(2,1)} %wk_hbm.1, bf16[64,1024]{1,0:T(8,128)(2,1)} %wv_hbm.1, ...), custom_call_target="tpu_custom_call" | custom-call | tf_op jit(solution)/shard_map/pallas_call | solution.py:552
  53.7 1.5 %shard_map.96 = (bf16[256,1024]{1,0:T(8,128)(2,1)}, f32[1024,512]{1,0:T(8,128)}) custom-call(bf16[256,1024]{1,0:T(8,128)(2,1)S(1)} %get-tuple-element.6.att, f32[1024,512]{1,0:T(8,128)S(1)} %get-tuple-element.7.d_neigh), custom_call_target="tpu_custom_call" | custom-call | tf_op jit(solution)/shard_map/pallas_call | solution.py:597
